TPU v7x, 32 devices: a whole 2x2x4 slice. The times are simulated.
32 devices in a mesh: gx: 4 (over y, x), gy: 2 (over core), gz: 4 (over z).
Axes of the slice: x: 2, y: 2, z: 4, core: 2. Of those that a mesh axis runs over, the one named last changes fastest.
Arguments:
- residual_in: float32 [256, 128, 1024], P('gx', 'gy', 'gz'), may hold values from -700 to 700
Outputs:
- level_one: float32 [128, 64, 512], P('gx', 'gy', 'gz')
- level_two: float32 [64, 32, 256], P('gx', 'gy', 'gz')
- level_three: float32 [32, 16, 128], P('gx', 'gy', 'gz')
- level_four: float32 [16, 8, 64], P('gx', 'gy', 'gz')
- level_five: float32 [8, 4, 32], P('gx', 'gy', 'gz')
- level_scales: float32 [5], replicated
All inputs are finite; a program needn't handle non-finite values.
Results may differ from a plain program's by a relative error of at most 0.0002.
Values sent between devices are 32-bit elements; how exact they have to be, the bound alone decides.
A program may use at most 64 MiB of HBM per device.

v0:
```python
import jax
import jax.numpy as jnp
from jax import lax
from jax.sharding import PartitionSpec as P

LEVELS = 5
EPSILON = 1e-06


def shifted(block, axis, distance):
    devices = range(lax.axis_size(axis))
    route = [(i - distance, i) for i in devices if i - distance in devices]
    return lax.ppermute(block, axis, route)


def pass_axis(values, axis_pos, rim_plane):
    length = values.shape[axis_pos]
    half = length // 2
    if axis_pos == 2:
        rows = lax.broadcasted_iota(jnp.int32, (length, half), 0)
        cols = lax.broadcasted_iota(jnp.int32, (length, half), 1)
        table = jnp.where(
            rows == 2 * cols,
            0.5,
            jnp.where((rows == 2 * cols + 1) | (rows == 2 * cols - 1), 0.25, 0.0),
        ).astype(jnp.float32)
        reduced = lax.dot_general(
            values,
            table,
            (((2,), (0,)), ((), ())),
            precision=lax.Precision.HIGHEST,
            preferred_element_type=jnp.float32,
        )
        tail = jnp.zeros(values.shape[:2] + (half - 1,), jnp.float32)
        return reduced + jnp.concatenate([0.25 * rim_plane, tail], axis=2)
    new_shape = values.shape[:axis_pos] + (half, 2) + values.shape[axis_pos + 1 :]
    paired = values.reshape(new_shape)
    even_part = lax.index_in_dim(paired, 0, axis_pos + 1, False)
    odd_part = lax.index_in_dim(paired, 1, axis_pos + 1, False)
    earlier = jnp.concatenate(
        [rim_plane, lax.slice_in_dim(odd_part, 0, half - 1, 1, axis_pos)], axis=axis_pos
    )
    return 0.5 * even_part + 0.25 * odd_part + 0.25 * earlier


def extend_cube(values):
    plane_x = shifted(values[-1:, :, :], "gx", 1)
    values = jnp.concatenate([plane_x, values], axis=0)
    plane_y = shifted(values[:, -1:, :], "gy", 1)
    values = jnp.concatenate([plane_y, values], axis=1)
    plane_z = shifted(values[:, :, -1:], "gz", 1)
    return jnp.concatenate([plane_z, values], axis=2)


def combine_cube(padded):
    values = pass_axis(padded[1:], 0, padded[:1])
    values = pass_axis(values[:, 1:], 1, values[:, :1])
    return pass_axis(values[:, :, 1:], 2, values[:, :, :1])


def restrict_any(values):
    return combine_cube(extend_cube(values))


def per_device(residual_in):
    devices_all = lax.axis_size("gx") * lax.axis_size("gy") * lax.axis_size("gz")
    current = residual_in
    grid_list = []
    scale_list = []
    unscaled = []
    sums_local = []
    for step_no in range(LEVELS):
        coarse = restrict_any(current)
        sums_local.append(jnp.sum(coarse * coarse))
        unscaled.append(coarse)
        current = coarse
    totals = lax.psum(jnp.stack(sums_local), ("gx", "gy", "gz"))
    product = jnp.float32(1.0)
    for step_no in range(LEVELS):
        cells = unscaled[step_no].size * devices_all
        scale_now = jnp.sqrt(totals[step_no] / (product * product) / cells + EPSILON)
        product = product * scale_now
        grid_list.append(unscaled[step_no] / product)
        scale_list.append(scale_now)
    return (
        grid_list[0],
        grid_list[1],
        grid_list[2],
        grid_list[3],
        grid_list[4],
        jnp.stack(scale_list),
    )


def solution(mesh):
    placed = (P("gx", "gy", "gz"),)
    return jax.shard_map(
        per_device,
        mesh=mesh,
        in_specs=placed,
        out_specs=(
            P("gx", "gy", "gz"),
            P("gx", "gy", "gz"),
            P("gx", "gy", "gz"),
            P("gx", "gy", "gz"),
            P("gx", "gy", "gz"),
            P(),
        ),
        check_vma=False,
    )
```

profile of v0, /device:TPU:0, one launch (start us, length us, event | category | flops | bytes accessed | tf_op | source)
XLA Modules:
  0.0 157.5 jit_solution(14000450861790597113)
XLA Ops:
  1.5 4.9 %collective-permute-start = (f32[1,64,256]{2,1,0:T(8,128)S(1)}, f32[1,64,256]{2,1,0:T(8,128)S(1)}, u32[]{:S(2)}, u32[]{:S(2)}) collective-permute-start(f32[1,64,256]{2,1,0:T(8,128)S(1)} %slice.260), channel_id=1, source_target_pairs={{0,8},{8,16},{16,24},{1,9},{9,17},{17,25},{2,10},{10,18},{18,26},{... | collective-permute-start | bytes 196616 | tf_op jit(solution)/shard_map/ppermute | solution.py:13
  6.3 1.9 %collective-permute-done = f32[1,64,256]{2,1,0:T(8,128)S(1)} collective-permute-done((f32[1,64,256]{2,1,0:T(8,128)S(1)}, f32[1,64,256]{2,1,0:T(8,128)S(1)}, u32[]{:S(2)}, u32[]{:S(2)}) %collective-permute-start) | collective-permute-done | bytes 65568 | tf_op jit(solution)/shard_map/ppermute | solution.py:13
  8.2 3.0 %constant_dynamic-update-slice_fusion = f32[65,64,256]{2,1,0:T(8,128)S(1)} fusion(f32[65,64,256]{2,1,0:T(8,128)S(1)} %constant_dynamic-update-slice_fusion.1, f32[64,64,256]{2,1,0:T(8,128)} %param.1), kind=kLoop, calls=%fused_computation.182 | loop fusion | bytes 8388608 | tf_op jit(solution)/shard_map/concatenate | solution.py:48
  11.3 1.3 collective-permute-start.1
  15.1 3.5 %collective-permute-start.2 = (f32[65,65,1]{1,2,0:T(1,128)S(1)}, f32[65,65,1]{1,2,0:T(1,128)S(1)}, u32[]{:S(2)}, u32[]{:S(2)}) collective-permute-start(f32[65,65,1]{1,2,0:T(1,128)S(1)} %copy.49), channel_id=1, source_target_pairs={{0,1},{1,2},{2,3},{4,5},{5,6},{6,7},{8,9},{9,10},{10,11},{12,13},{... | collective-permute-start | bytes 50708 | tf_op jit(solution)/shard_map/ppermute | solution.py:13
  18.6 1.6 collective-permute-done.2
  21.1 4.7 %maximum_maximum_fusion = f32[65,65,257]{2,1,0:T(8,128)S(1)} fusion(f32[65,64,256]{2,1,0:T(8,128)} %copy-done, f32[65,1,256]{2,1,0:T(1,128)S(1)} %collective-permute-done.1, f32[65,65,1]{2,1,0:T(8,128)S(1)} %copy.50), kind=kLoop, calls=%fused_computation | loop fusion | flops 2171650 | bytes 8686600 | tf_op jit(solution)/shard_map/concatenate | solution.py:52
  26.6 2.1 %fusion.2 = f32[32,65,257]{2,1,0:T(8,128)S(1)} fusion(f32[65,65,1]{2,1,0:T(8,128)S(1)} %copy.50, f32[65,64,256]{2,1,0:T(8,128)S(1)} %bitcast.209, f32[65,1,256]{2,1,0:T(1,128)S(1)} %collective-permute-done.1, f32[32,2,65,257]{3,2,1,0:T(8,128)S(1)} %bitcast.207, f32[31,65,257]{2,1,0:T(8,128)S(1)} %slice_bitcast_fusion.2), kind=kLoop, calls=%fused_computation.4 | loop fusion | flops 6414720 | bytes 12829440 | tf_op jit(solution)/shard_map/add | solution.py:43
  29.2 1.8 %copy.55 = f32[32,64,257]{2,0,1:T(8,128)S(1)} copy(f32[32,64,257]{2,1,0:T(8,128)S(1)} %slice.350) | data formatting | bytes 4210688 | tf_op jit(solution)/shard_map/slice | solution.py:57
  32.2 2.0 %fusion.10 = f32[32,32,257]{2,1,0:T(8,128)S(1)} fusion(f32[32,31,257]{2,1,0:T(8,128)S(1)} %bitcast.213, f32[32,1,257]{2,1,0:T(1,128)S(1)} %slice.353, f32[32,32,1,257]{3,0,2,1:T(8,128)S(1)} %get-tuple-element.6, f32[32,32,1,257]{3,0,2,1:T(8,128)S(1)} %get-tuple-element.7), kind=kLoop, calls=%fused_computation.18 | loop fusion | flops 1579008 | bytes 4210688 | tf_op jit(solution)/shard_map/add | solution.py:43
  34.2 1.6 %multiply_reduce_fusion = (f32[]{:T(128)}, f32[32,32,128]{2,1,0:T(8,128)S(1)}) fusion(f32[32,32,1]{2,1,0:T(8,128)S(1)} %slice_multiply_fusion, s32[128]{0:T(128)S(1)} %get-tuple-element.34, s32[128]{0:T(128)S(1)} %broadcast_add_fusion.9, s32[128]{0:T(128)S(1)} %get-tuple-element.33, f32[32,32,257]{2,1,0:T(8,128)S(1)} %fusion.10), kind=kOutput, calls=%fused_computation.49 | convolution fusion | flops 403243008 | bytes 2098692 | tf_op jit(solution)/shard_map/dot_general | solution.py:27
  35.9 4.3 %collective-permute-start.3 = (f32[1,32,128]{2,1,0:T(8,128)S(1)}, f32[1,32,128]{2,1,0:T(8,128)S(1)}, u32[]{:S(2)}, u32[]{:S(2)}) collective-permute-start(f32[1,32,128]{2,1,0:T(8,128)S(1)} %slice.357), channel_id=1, source_target_pairs={{0,8},{8,16},{16,24},{1,9},{9,17},{17,25},{2,10},{10,18},{18,26},{... | collective-permute-start | bytes 49160 | tf_op jit(solution)/shard_map/ppermute | solution.py:13
  40.1 1.4 collective-permute-done.3
  41.6 1.3 collective-permute-start.4
  44.3 4.4 %collective-permute-start.5 = (f32[33,33,1]{1,2,0:T(1,128)S(1)}, f32[33,33,1]{1,2,0:T(1,128)S(1)}, u32[]{:S(2)}, u32[]{:S(2)}) collective-permute-start(f32[33,33,1]{1,2,0:T(1,128)S(1)} %copy.58), channel_id=1, source_target_pairs={{0,1},{1,2},{2,3},{4,5},{5,6},{6,7},{8,9},{9,10},{10,11},{12,13},{... | collective-permute-start | bytes 13076 | tf_op jit(solution)/shard_map/ppermute | solution.py:13
  53.0 4.3 %collective-permute-start.6 = (f32[1,16,64]{2,1,0:T(8,128)S(1)}, f32[1,16,64]{2,1,0:T(8,128)S(1)}, u32[]{:S(2)}, u32[]{:S(2)}) collective-permute-start(f32[1,16,64]{2,1,0:T(8,128)S(1)} %slice.369), channel_id=1, source_target_pairs={{0,8},{8,16},{16,24},{1,9},{9,17},{17,25},{2,10},{10,18},{18,26},{... | collective-permute-start | bytes 12296 | tf_op jit(solution)/shard_map/ppermute | solution.py:13
  57.3 1.3 collective-permute-done.6
  58.7 1.3 collective-permute-start.7
  60.9 4.2 %collective-permute-start.8 = (f32[17,17,1]{2,1,0:T(8,128)S(1)}, f32[17,17,1]{2,1,0:T(8,128)S(1)}, u32[]{:S(2)}, u32[]{:S(2)}) collective-permute-start(f32[17,17,1]{2,1,0:T(8,128)S(1)} %pad_maximum_fusion.3), channel_id=1, source_target_pairs={{0,1},{1,2},{2,3},{4,5},{5,6},{6,7},{8,9},{9,10},{10,11},{12,13},{... | collective-permute-start | bytes 3476 | tf_op jit(solution)/shard_map/ppermute | solution.py:13
  65.1 4.9 %collective-permute-done.8 = f32[17,17,1]{2,1,0:T(8,128)S(1)} collective-permute-done((f32[17,17,1]{2,1,0:T(8,128)S(1)}, f32[17,17,1]{2,1,0:T(8,128)S(1)}, u32[]{:S(2)}, u32[]{:S(2)}) %collective-permute-start.8) | collective-permute-done | bytes 1188 | tf_op jit(solution)/shard_map/ppermute | solution.py:13
  71.3 5.1 %collective-permute-start.9 = (f32[1,8,32]{2,1,0:T(8,128)S(1)}, f32[1,8,32]{2,1,0:T(8,128)S(1)}, u32[]{:S(2)}, u32[]{:S(2)}) collective-permute-start(f32[1,8,32]{2,1,0:T(8,128)S(1)} %slice.381), channel_id=1, source_target_pairs={{0,8},{8,16},{16,24},{1,9},{9,17},{17,25},{2,10},{10,18},{18,26},{... | collective-permute-start | bytes 3080 | tf_op jit(solution)/shard_map/ppermute | solution.py:13
  76.4 1.3 collective-permute-done.9
  77.7 1.3 collective-permute-start.10
  79.9 4.4 %collective-permute-start.11 = (f32[9,9,1]{2,1,0:T(8,128)S(1)}, f32[9,9,1]{2,1,0:T(8,128)S(1)}, u32[]{:S(2)}, u32[]{:S(2)}) collective-permute-start(f32[9,9,1]{2,1,0:T(8,128)S(1)} %pad_maximum_fusion.5), channel_id=1, source_target_pairs={{0,1},{1,2},{2,3},{4,5},{5,6},{6,7},{8,9},{9,10},{10,11},{12,13},{... | collective-permute-start | bytes 980 | tf_op jit(solution)/shard_map/ppermute | solution.py:13
  84.3 2.0 %collective-permute-done.11 = f32[9,9,1]{2,1,0:T(8,128)S(1)} collective-permute-done((f32[9,9,1]{2,1,0:T(8,128)S(1)}, f32[9,9,1]{2,1,0:T(8,128)S(1)}, u32[]{:S(2)}, u32[]{:S(2)}) %collective-permute-start.11) | collective-permute-done | bytes 356 | tf_op jit(solution)/shard_map/ppermute | solution.py:13
  87.5 5.1 %collective-permute-start.12 = (f32[1,4,16]{2,1,0:T(4,128)S(1)}, f32[1,4,16]{2,1,0:T(4,128)S(1)}, u32[]{:S(2)}, u32[]{:S(2)}) collective-permute-start(f32[1,4,16]{2,1,0:T(4,128)S(1)} %slice.393), channel_id=1, source_target_pairs={{0,8},{8,16},{16,24},{1,9},{9,17},{17,25},{2,10},{10,18},{18,26},{... | collective-permute-start | bytes 776 | tf_op jit(solution)/shard_map/ppermute | solution.py:13
  92.5 1.3 collective-permute-done.12
  93.8 1.3 collective-permute-start.13
  96.0 4.4 %collective-permute-start.14 = (f32[5,5,1]{2,1,0:T(8,128)S(1)}, f32[5,5,1]{2,1,0:T(8,128)S(1)}, u32[]{:S(2)}, u32[]{:S(2)}) collective-permute-start(f32[5,5,1]{2,1,0:T(8,128)S(1)} %pad_maximum_fusion.7), channel_id=1, source_target_pairs={{0,1},{1,2},{2,3},{4,5},{5,6},{6,7},{8,9},{9,10},{10,11},{12,13},{... | collective-permute-start | bytes 308 | tf_op jit(solution)/shard_map/ppermute | solution.py:13
  100.4 1.5 collective-permute-done.14
  103.0 3.3 %stack.39 = f32[5]{0:T(128)S(1)} concatenate(f32[1]{0:T(128)} %bitcast.7, f32[1]{0:T(128)} %bitcast.15, f32[1]{0:T(128)} %bitcast.23, f32[1]{0:T(128)} %bitcast.31, f32[1]{0:T(128)} %bitcast.39), dimensions={0} | concatenate | bytes 40 | tf_op jit(solution)/shard_map/stack | solution.py:77
  106.3 43.1 %psum.7 = f32[5]{0:T(128)S(1)} all-reduce(f32[5]{0:T(128)S(1)} %stack.39), channel_id=1, replica_groups=mesh['gx'=4,'gy'=2,'gz'=4] {'gx','gy','gz'}, use_global_device_ids=true, to_apply=%region_5.6 | all-reduce | flops 5 | bytes 40 | tf_op jit(solution)/shard_map/psum | solution.py:77
  (105 shorter events, 23.0 us)
Async XLA Ops:
  1.5 6.8 %collective-permute-start = (f32[1,64,256]{2,1,0:T(8,128)S(1)}, f32[1,64,256]{2,1,0:T(8,128)S(1)}, u32[]{:S(2)}, u32[]{:S(2)}) collective-permute-start(f32[1,64,256]{2,1,0:T(8,128)S(1)} %slice.260), channel_id=1, source_target_pairs={{0,8},{8,16},{16,24},{1,9},{9,17},{17,25},{2,10},{10,18},{18,26},{... | collective-permute-start | bytes 196616 | tf_op jit(solution)/shard_map/ppermute | solution.py:13
  11.2 2.3 %copy-start = (f32[65,64,256]{2,1,0:T(8,128)}, f32[65,64,256]{2,1,0:T(8,128)S(1)}, u32[]{:S(2)}) copy-start(f32[65,64,256]{2,1,0:T(8,128)S(1)} %constant_dynamic-update-slice_fusion) | copy-start | bytes 12779524
  11.3 2.2 %collective-permute-start.1 = (f32[65,1,256]{2,1,0:T(1,128)S(1)}, f32[65,1,256]{2,1,0:T(1,128)S(1)}, u32[]{:S(2)}, u32[]{:S(2)}) collective-permute-start(f32[65,1,256]{2,1,0:T(1,128)S(1)} %slice.345), channel_id=1, source_target_pairs={{0,4},{1,5},{2,6},{3,7},{8,12},{9,13},{10,14},{11,15},{16,20},{17,... | collective-permute-start | bytes 199688 | tf_op jit(solution)/shard_map/ppermute | solution.py:13
  15.1 5.1 %collective-permute-start.2 = (f32[65,65,1]{1,2,0:T(1,128)S(1)}, f32[65,65,1]{1,2,0:T(1,128)S(1)}, u32[]{:S(2)}, u32[]{:S(2)}) collective-permute-start(f32[65,65,1]{1,2,0:T(1,128)S(1)} %copy.49), channel_id=1, source_target_pairs={{0,1},{1,2},{2,3},{4,5},{5,6},{6,7},{8,9},{9,10},{10,11},{12,13},{... | collective-permute-start | bytes 50708 | tf_op jit(solution)/shard_map/ppermute | solution.py:13
  21.1 5.4 %slice-start = ((s8[4259840]{0:T(1024)(128)(4,1)}), s8[4194304]{0:T(1024)(128)(4,1)S(1)}, s32[]{:S(2)}) async-start(s8[4259840]{0:T(1024)(128)(4,1)} %bitcast.208), calls=%async_computation | async-start | bytes 8388608
  25.8 0.8 slice-start.1
  35.9 5.7 %collective-permute-start.3 = (f32[1,32,128]{2,1,0:T(8,128)S(1)}, f32[1,32,128]{2,1,0:T(8,128)S(1)}, u32[]{:S(2)}, u32[]{:S(2)}) collective-permute-start(f32[1,32,128]{2,1,0:T(8,128)S(1)} %slice.357), channel_id=1, source_target_pairs={{0,8},{8,16},{16,24},{1,9},{9,17},{17,25},{2,10},{10,18},{18,26},{... | collective-permute-start | bytes 49160 | tf_op jit(solution)/shard_map/ppermute | solution.py:13
  41.6 2.1 %collective-permute-start.4 = (f32[33,1,128]{2,1,0:T(1,128)S(1)}, f32[33,1,128]{2,1,0:T(1,128)S(1)}, u32[]{:S(2)}, u32[]{:S(2)}) collective-permute-start(f32[33,1,128]{2,1,0:T(1,128)S(1)} %pad_maximum_fusion.9), channel_id=1, source_target_pairs={{0,4},{1,5},{2,6},{3,7},{8,12},{9,13},{10,14},{11,15},{16,20},{17,... | collective-permute-start | bytes 50696 | tf_op jit(solution)/shard_map/ppermute | solution.py:13
  44.3 5.7 %collective-permute-start.5 = (f32[33,33,1]{1,2,0:T(1,128)S(1)}, f32[33,33,1]{1,2,0:T(1,128)S(1)}, u32[]{:S(2)}, u32[]{:S(2)}) collective-permute-start(f32[33,33,1]{1,2,0:T(1,128)S(1)} %copy.58), channel_id=1, source_target_pairs={{0,1},{1,2},{2,3},{4,5},{5,6},{6,7},{8,9},{9,10},{10,11},{12,13},{... | collective-permute-start | bytes 13076 | tf_op jit(solution)/shard_map/ppermute | solution.py:13
  53.0 5.6 %collective-permute-start.6 = (f32[1,16,64]{2,1,0:T(8,128)S(1)}, f32[1,16,64]{2,1,0:T(8,128)S(1)}, u32[]{:S(2)}, u32[]{:S(2)}) collective-permute-start(f32[1,16,64]{2,1,0:T(8,128)S(1)} %slice.369), channel_id=1, source_target_pairs={{0,8},{8,16},{16,24},{1,9},{9,17},{17,25},{2,10},{10,18},{18,26},{... | collective-permute-start | bytes 12296 | tf_op jit(solution)/shard_map/ppermute | solution.py:13
  58.7 2.1 %collective-permute-start.7 = (f32[17,1,64]{2,1,0:T(1,128)S(1)}, f32[17,1,64]{2,1,0:T(1,128)S(1)}, u32[]{:S(2)}, u32[]{:S(2)}) collective-permute-start(f32[17,1,64]{2,1,0:T(1,128)S(1)} %pad_maximum_fusion.10), channel_id=1, source_target_pairs={{0,4},{1,5},{2,6},{3,7},{8,12},{9,13},{10,14},{11,15},{16,20},{17,... | collective-permute-start | bytes 13064 | tf_op jit(solution)/shard_map/ppermute | solution.py:13
  60.9 9.1 %collective-permute-start.8 = (f32[17,17,1]{2,1,0:T(8,128)S(1)}, f32[17,17,1]{2,1,0:T(8,128)S(1)}, u32[]{:S(2)}, u32[]{:S(2)}) collective-permute-start(f32[17,17,1]{2,1,0:T(8,128)S(1)} %pad_maximum_fusion.3), channel_id=1, source_target_pairs={{0,1},{1,2},{2,3},{4,5},{5,6},{6,7},{8,9},{9,10},{10,11},{12,13},{... | collective-permute-start | bytes 3476 | tf_op jit(solution)/shard_map/ppermute | solution.py:13
  71.3 6.4 %collective-permute-start.9 = (f32[1,8,32]{2,1,0:T(8,128)S(1)}, f32[1,8,32]{2,1,0:T(8,128)S(1)}, u32[]{:S(2)}, u32[]{:S(2)}) collective-permute-start(f32[1,8,32]{2,1,0:T(8,128)S(1)} %slice.381), channel_id=1, source_target_pairs={{0,8},{8,16},{16,24},{1,9},{9,17},{17,25},{2,10},{10,18},{18,26},{... | collective-permute-start | bytes 3080 | tf_op jit(solution)/shard_map/ppermute | solution.py:13
  77.7 2.1 %collective-permute-start.10 = (f32[9,1,32]{2,1,0:T(1,128)S(1)}, f32[9,1,32]{2,1,0:T(1,128)S(1)}, u32[]{:S(2)}, u32[]{:S(2)}) collective-permute-start(f32[9,1,32]{2,1,0:T(1,128)S(1)} %pad_maximum_fusion.11), channel_id=1, source_target_pairs={{0,4},{1,5},{2,6},{3,7},{8,12},{9,13},{10,14},{11,15},{16,20},{17,... | collective-permute-start | bytes 3464 | tf_op jit(solution)/shard_map/ppermute | solution.py:13
  79.9 6.4 %collective-permute-start.11 = (f32[9,9,1]{2,1,0:T(8,128)S(1)}, f32[9,9,1]{2,1,0:T(8,128)S(1)}, u32[]{:S(2)}, u32[]{:S(2)}) collective-permute-start(f32[9,9,1]{2,1,0:T(8,128)S(1)} %pad_maximum_fusion.5), channel_id=1, source_target_pairs={{0,1},{1,2},{2,3},{4,5},{5,6},{6,7},{8,9},{9,10},{10,11},{12,13},{... | collective-permute-start | bytes 980 | tf_op jit(solution)/shard_map/ppermute | solution.py:13
  87.5 6.4 %collective-permute-start.12 = (f32[1,4,16]{2,1,0:T(4,128)S(1)}, f32[1,4,16]{2,1,0:T(4,128)S(1)}, u32[]{:S(2)}, u32[]{:S(2)}) collective-permute-start(f32[1,4,16]{2,1,0:T(4,128)S(1)} %slice.393), channel_id=1, source_target_pairs={{0,8},{8,16},{16,24},{1,9},{9,17},{17,25},{2,10},{10,18},{18,26},{... | collective-permute-start | bytes 776 | tf_op jit(solution)/shard_map/ppermute | solution.py:13
  93.8 2.1 %collective-permute-start.13 = (f32[5,1,16]{2,1,0:T(1,128)S(1)}, f32[5,1,16]{2,1,0:T(1,128)S(1)}, u32[]{:S(2)}, u32[]{:S(2)}) collective-permute-start(f32[5,1,16]{2,1,0:T(1,128)S(1)} %pad_maximum_fusion.12), channel_id=1, source_target_pairs={{0,4},{1,5},{2,6},{3,7},{8,12},{9,13},{10,14},{11,15},{16,20},{17,... | collective-permute-start | bytes 968 | tf_op jit(solution)/shard_map/ppermute | solution.py:13
  96.0 5.9 %collective-permute-start.14 = (f32[5,5,1]{2,1,0:T(8,128)S(1)}, f32[5,5,1]{2,1,0:T(8,128)S(1)}, u32[]{:S(2)}, u32[]{:S(2)}) collective-permute-start(f32[5,5,1]{2,1,0:T(8,128)S(1)} %pad_maximum_fusion.7), channel_id=1, source_target_pairs={{0,1},{1,2},{2,3},{4,5},{5,6},{6,7},{8,9},{9,10},{10,11},{12,13},{... | collective-permute-start | bytes 308 | tf_op jit(solution)/shard_map/ppermute | solution.py:13
where the time goes:
time: 158 us; the launch traced here: 157 us
  starting transfers between devices  50.9 us (32%)
  blocking collectives  43.1 us (27%)
  waiting for transfers between devices  22.5 us (14%)
  local copies, waits for them, and re-layouts  15.9 us (10%)
  other arithmetic  15.3 us (10%)
  matrix products  5.1 us (3%)
  between operations  4.72 us (3%)
    ppermute x15, starting transfers between devices, shifted(): return lax.ppermute(block, axis, route)  50.9 us
    psum x1, blocking collectives, per_device(): totals = lax.psum(jnp.stack(sums_local), ('gx', 'gy', 'gz'))  43.1 us
    ppermute x15, waiting for transfers between devices, shifted(): return lax.ppermute(block, axis, route)  22.5 us
    concatenate x5, other arithmetic, extend_cube(): return jnp.concatenate([plane_z, values], axis=2)  5.51 us
    dot_general x5, matrix products, pass_axis(): lax.dot_general(values, table, (((2,), (0,)), ((), ())), precision=lax.Pr...  5.1 us
    add x10, other arithmetic, pass_axis(): return 0.5 * even_part + 0.25 * odd_part + 0.25 * earlier  4.91 us
    div x5, other arithmetic, per_device(): grid_list.append(unscaled[step_no] / product)  3.34 us
    another operation x1, local copies, waits for them, and re-layouts, per_device(): totals = lax.psum(jnp.stack(sums_local), ('gx', 'gy', 'gz'))  3.31 us
  transfers between devices with their start and end apart: 15, of which 15 were waited for; matrix products, arithmetic and copies ran while one was open for 0% of the time, Pallas kernels for 0%

commit v1 on v0

--- a/solution.py
+++ b/solution.py
@@ -74,7 +74,8 @@
         sums_local.append(jnp.sum(coarse * coarse))
         unscaled.append(coarse)
         current = coarse
-    totals = lax.psum(jnp.stack(sums_local), ("gx", "gy", "gz"))
+    _number_circles = lambda unit, across, net_axis: lax.psum(lax.psum(unit, across), net_axis)
+    totals = _number_circles(jnp.stack(sums_local), ("gy", "gz"), "gx")
     product = jnp.float32(1.0)
     for step_no in range(LEVELS):
         cells = unscaled[step_no].size * devices_all

time: 158 us -> 143 us (0.905)
  blocking collectives: 43.1 us -> 27.7 us
    psum x1 -> x2, blocking collectives: 43.1 us -> 27.7 us  [the longest x1 16.8 us: per_device(): lax.psum(unit, across)]
where the time goes in v1:
time: 143 us; the launch traced here: 142 us
  starting transfers between devices  50.9 us (36%)
  blocking collectives  27.7 us (19%)
  waiting for transfers between devices  22.5 us (16%)
  local copies, waits for them, and re-layouts  15.9 us (11%)
  other arithmetic  15.3 us (11%)
  matrix products  5.1 us (4%)
  between operations  4.72 us (3%)
    ppermute x15, starting transfers between devices, shifted(): return lax.ppermute(block, axis, route)  50.9 us
    ppermute x15, waiting for transfers between devices, shifted(): return lax.ppermute(block, axis, route)  22.5 us
    psum x1, blocking collectives, per_device(): lax.psum(unit, across)  16.8 us
    psum x1, blocking collectives, per_device(): lax.psum(lax.psum(unit, across), net_axis)  10.9 us
    concatenate x5, other arithmetic, extend_cube(): return jnp.concatenate([plane_z, values], axis=2)  5.51 us
    dot_general x5, matrix products, pass_axis(): lax.dot_general(values, table, (((2,), (0,)), ((), ())), precision=lax.Pr...  5.1 us
    add x10, other arithmetic, pass_axis(): return 0.5 * even_part + 0.25 * odd_part + 0.25 * earlier  4.91 us
    div x5, other arithmetic, per_device(): grid_list.append(unscaled[step_no] / product)  3.34 us
  transfers between devices with their start and end apart: 15, of which 15 were waited for; matrix products, arithmetic and copies ran while one was open for 0% of the time, Pallas kernels for 0%

profile of v1, /device:TPU:0, one launch (start us, length us, event | category | flops | bytes accessed | tf_op | source)
XLA Modules:
  0.0 142.0 jit_solution(15272526762301315228)
XLA Ops:
  1.5 4.9 %collective-permute-start = (f32[1,64,256]{2,1,0:T(8,128)S(1)}, f32[1,64,256]{2,1,0:T(8,128)S(1)}, u32[]{:S(2)}, u32[]{:S(2)}) collective-permute-start(f32[1,64,256]{2,1,0:T(8,128)S(1)} %slice.260), channel_id=1, source_target_pairs={{0,8},{8,16},{16,24},{1,9},{9,17},{17,25},{2,10},{10,18},{18,26},{... | collective-permute-start | bytes 196616 | tf_op jit(solution)/shard_map/ppermute | solution.py:13
  6.3 1.9 %collective-permute-done = f32[1,64,256]{2,1,0:T(8,128)S(1)} collective-permute-done((f32[1,64,256]{2,1,0:T(8,128)S(1)}, f32[1,64,256]{2,1,0:T(8,128)S(1)}, u32[]{:S(2)}, u32[]{:S(2)}) %collective-permute-start) | collective-permute-done | bytes 65568 | tf_op jit(solution)/shard_map/ppermute | solution.py:13
  8.2 3.0 %constant_dynamic-update-slice_fusion = f32[65,64,256]{2,1,0:T(8,128)S(1)} fusion(f32[65,64,256]{2,1,0:T(8,128)S(1)} %constant_dynamic-update-slice_fusion.1, f32[64,64,256]{2,1,0:T(8,128)} %param.1), kind=kLoop, calls=%fused_computation.182 | loop fusion | bytes 8388608 | tf_op jit(solution)/shard_map/concatenate | solution.py:48
  11.3 1.3 collective-permute-start.1
  15.1 3.5 %collective-permute-start.2 = (f32[65,65,1]{1,2,0:T(1,128)S(1)}, f32[65,65,1]{1,2,0:T(1,128)S(1)}, u32[]{:S(2)}, u32[]{:S(2)}) collective-permute-start(f32[65,65,1]{1,2,0:T(1,128)S(1)} %copy.49), channel_id=1, source_target_pairs={{0,1},{1,2},{2,3},{4,5},{5,6},{6,7},{8,9},{9,10},{10,11},{12,13},{... | collective-permute-start | bytes 50708 | tf_op jit(solution)/shard_map/ppermute | solution.py:13
  18.6 1.6 %collective-permute-done.2 = f32[65,65,1]{1,2,0:T(1,128)S(1)} collective-permute-done((f32[65,65,1]{1,2,0:T(1,128)S(1)}, f32[65,65,1]{1,2,0:T(1,128)S(1)}, u32[]{:S(2)}, u32[]{:S(2)}) %collective-permute-start.2) | collective-permute-done | bytes 16932 | tf_op jit(solution)/shard_map/ppermute | solution.py:13
  21.1 4.7 %maximum_maximum_fusion = f32[65,65,257]{2,1,0:T(8,128)S(1)} fusion(f32[65,64,256]{2,1,0:T(8,128)} %copy-done, f32[65,1,256]{2,1,0:T(1,128)S(1)} %collective-permute-done.1, f32[65,65,1]{2,1,0:T(8,128)S(1)} %copy.50), kind=kLoop, calls=%fused_computation | loop fusion | flops 2171650 | bytes 8686600 | tf_op jit(solution)/shard_map/concatenate | solution.py:52
  26.6 2.1 %fusion.2 = f32[32,65,257]{2,1,0:T(8,128)S(1)} fusion(f32[65,65,1]{2,1,0:T(8,128)S(1)} %copy.50, f32[65,64,256]{2,1,0:T(8,128)S(1)} %bitcast.209, f32[65,1,256]{2,1,0:T(1,128)S(1)} %collective-permute-done.1, f32[32,2,65,257]{3,2,1,0:T(8,128)S(1)} %bitcast.207, f32[31,65,257]{2,1,0:T(8,128)S(1)} %slice_bitcast_fusion.2), kind=kLoop, calls=%fused_computation.4 | loop fusion | flops 6414720 | bytes 12829440 | tf_op jit(solution)/shard_map/add | solution.py:43
  29.2 1.8 %copy.55 = f32[32,64,257]{2,0,1:T(8,128)S(1)} copy(f32[32,64,257]{2,1,0:T(8,128)S(1)} %slice.350) | data formatting | bytes 4210688 | tf_op jit(solution)/shard_map/slice | solution.py:57
  32.2 2.0 %fusion.10 = f32[32,32,257]{2,1,0:T(8,128)S(1)} fusion(f32[32,31,257]{2,1,0:T(8,128)S(1)} %bitcast.213, f32[32,1,257]{2,1,0:T(1,128)S(1)} %slice.353, f32[32,32,1,257]{3,0,2,1:T(8,128)S(1)} %get-tuple-element.6, f32[32,32,1,257]{3,0,2,1:T(8,128)S(1)} %get-tuple-element.7), kind=kLoop, calls=%fused_computation.18 | loop fusion | flops 1579008 | bytes 4210688 | tf_op jit(solution)/shard_map/add | solution.py:43
  34.2 1.6 %multiply_reduce_fusion = (f32[]{:T(128)}, f32[32,32,128]{2,1,0:T(8,128)S(1)}) fusion(f32[32,32,1]{2,1,0:T(8,128)S(1)} %slice_multiply_fusion, s32[128]{0:T(128)S(1)} %get-tuple-element.34, s32[128]{0:T(128)S(1)} %broadcast_add_fusion.9, s32[128]{0:T(128)S(1)} %get-tuple-element.33, f32[32,32,257]{2,1,0:T(8,128)S(1)} %fusion.10), kind=kOutput, calls=%fused_computation.49 | convolution fusion | flops 403243008 | bytes 2098692 | tf_op jit(solution)/shard_map/dot_general | solution.py:27
  35.9 4.3 %collective-permute-start.3 = (f32[1,32,128]{2,1,0:T(8,128)S(1)}, f32[1,32,128]{2,1,0:T(8,128)S(1)}, u32[]{:S(2)}, u32[]{:S(2)}) collective-permute-start(f32[1,32,128]{2,1,0:T(8,128)S(1)} %slice.357), channel_id=1, source_target_pairs={{0,8},{8,16},{16,24},{1,9},{9,17},{17,25},{2,10},{10,18},{18,26},{... | collective-permute-start | bytes 49160 | tf_op jit(solution)/shard_map/ppermute | solution.py:13
  40.1 1.4 %collective-permute-done.3 = f32[1,32,128]{2,1,0:T(8,128)S(1)} collective-permute-done((f32[1,32,128]{2,1,0:T(8,128)S(1)}, f32[1,32,128]{2,1,0:T(8,128)S(1)}, u32[]{:S(2)}, u32[]{:S(2)}) %collective-permute-start.3) | collective-permute-done | bytes 16416 | tf_op jit(solution)/shard_map/ppermute | solution.py:13
  41.6 1.3 collective-permute-start.4
  44.3 4.4 %collective-permute-start.5 = (f32[33,33,1]{1,2,0:T(1,128)S(1)}, f32[33,33,1]{1,2,0:T(1,128)S(1)}, u32[]{:S(2)}, u32[]{:S(2)}) collective-permute-start(f32[33,33,1]{1,2,0:T(1,128)S(1)} %copy.58), channel_id=1, source_target_pairs={{0,1},{1,2},{2,3},{4,5},{5,6},{6,7},{8,9},{9,10},{10,11},{12,13},{... | collective-permute-start | bytes 13076 | tf_op jit(solution)/shard_map/ppermute | solution.py:13
  53.0 4.3 %collective-permute-start.6 = (f32[1,16,64]{2,1,0:T(8,128)S(1)}, f32[1,16,64]{2,1,0:T(8,128)S(1)}, u32[]{:S(2)}, u32[]{:S(2)}) collective-permute-start(f32[1,16,64]{2,1,0:T(8,128)S(1)} %slice.369), channel_id=1, source_target_pairs={{0,8},{8,16},{16,24},{1,9},{9,17},{17,25},{2,10},{10,18},{18,26},{... | collective-permute-start | bytes 12296 | tf_op jit(solution)/shard_map/ppermute | solution.py:13
  57.3 1.3 collective-permute-done.6
  58.7 1.3 collective-permute-start.7
  60.9 4.2 %collective-permute-start.8 = (f32[17,17,1]{2,1,0:T(8,128)S(1)}, f32[17,17,1]{2,1,0:T(8,128)S(1)}, u32[]{:S(2)}, u32[]{:S(2)}) collective-permute-start(f32[17,17,1]{2,1,0:T(8,128)S(1)} %pad_maximum_fusion.3), channel_id=1, source_target_pairs={{0,1},{1,2},{2,3},{4,5},{5,6},{6,7},{8,9},{9,10},{10,11},{12,13},{... | collective-permute-start | bytes 3476 | tf_op jit(solution)/shard_map/ppermute | solution.py:13
  65.1 4.9 %collective-permute-done.8 = f32[17,17,1]{2,1,0:T(8,128)S(1)} collective-permute-done((f32[17,17,1]{2,1,0:T(8,128)S(1)}, f32[17,17,1]{2,1,0:T(8,128)S(1)}, u32[]{:S(2)}, u32[]{:S(2)}) %collective-permute-start.8) | collective-permute-done | bytes 1188 | tf_op jit(solution)/shard_map/ppermute | solution.py:13
  71.3 5.1 %collective-permute-start.9 = (f32[1,8,32]{2,1,0:T(8,128)S(1)}, f32[1,8,32]{2,1,0:T(8,128)S(1)}, u32[]{:S(2)}, u32[]{:S(2)}) collective-permute-start(f32[1,8,32]{2,1,0:T(8,128)S(1)} %slice.381), channel_id=1, source_target_pairs={{0,8},{8,16},{16,24},{1,9},{9,17},{17,25},{2,10},{10,18},{18,26},{... | collective-permute-start | bytes 3080 | tf_op jit(solution)/shard_map/ppermute | solution.py:13
  76.4 1.3 collective-permute-done.9
  77.7 1.3 collective-permute-start.10
  79.9 4.4 %collective-permute-start.11 = (f32[9,9,1]{2,1,0:T(8,128)S(1)}, f32[9,9,1]{2,1,0:T(8,128)S(1)}, u32[]{:S(2)}, u32[]{:S(2)}) collective-permute-start(f32[9,9,1]{2,1,0:T(8,128)S(1)} %pad_maximum_fusion.5), channel_id=1, source_target_pairs={{0,1},{1,2},{2,3},{4,5},{5,6},{6,7},{8,9},{9,10},{10,11},{12,13},{... | collective-permute-start | bytes 980 | tf_op jit(solution)/shard_map/ppermute | solution.py:13
  84.3 2.0 %collective-permute-done.11 = f32[9,9,1]{2,1,0:T(8,128)S(1)} collective-permute-done((f32[9,9,1]{2,1,0:T(8,128)S(1)}, f32[9,9,1]{2,1,0:T(8,128)S(1)}, u32[]{:S(2)}, u32[]{:S(2)}) %collective-permute-start.11) | collective-permute-done | bytes 356 | tf_op jit(solution)/shard_map/ppermute | solution.py:13
  87.5 5.1 %collective-permute-start.12 = (f32[1,4,16]{2,1,0:T(4,128)S(1)}, f32[1,4,16]{2,1,0:T(4,128)S(1)}, u32[]{:S(2)}, u32[]{:S(2)}) collective-permute-start(f32[1,4,16]{2,1,0:T(4,128)S(1)} %slice.393), channel_id=1, source_target_pairs={{0,8},{8,16},{16,24},{1,9},{9,17},{17,25},{2,10},{10,18},{18,26},{... | collective-permute-start | bytes 776 | tf_op jit(solution)/shard_map/ppermute | solution.py:13
  92.5 1.3 collective-permute-done.12
  96.0 4.4 %collective-permute-start.14 = (f32[5,5,1]{2,1,0:T(8,128)S(1)}, f32[5,5,1]{2,1,0:T(8,128)S(1)}, u32[]{:S(2)}, u32[]{:S(2)}) collective-permute-start(f32[5,5,1]{2,1,0:T(8,128)S(1)} %pad_maximum_fusion.7), channel_id=1, source_target_pairs={{0,1},{1,2},{2,3},{4,5},{5,6},{6,7},{8,9},{9,10},{10,11},{12,13},{... | collective-permute-start | bytes 308 | tf_op jit(solution)/shard_map/ppermute | solution.py:13
  100.4 1.5 %collective-permute-done.14 = f32[5,5,1]{2,1,0:T(8,128)S(1)} collective-permute-done((f32[5,5,1]{2,1,0:T(8,128)S(1)}, f32[5,5,1]{2,1,0:T(8,128)S(1)}, u32[]{:S(2)}, u32[]{:S(2)}) %collective-permute-start.14) | collective-permute-done | bytes 132 | tf_op jit(solution)/shard_map/ppermute | solution.py:13
  103.0 3.3 %stack.39 = f32[5]{0:T(128)S(1)} concatenate(f32[1]{0:T(128)} %bitcast.7, f32[1]{0:T(128)} %bitcast.15, f32[1]{0:T(128)} %bitcast.23, f32[1]{0:T(128)} %bitcast.31, f32[1]{0:T(128)} %bitcast.39), dimensions={0} | concatenate | bytes 40 | tf_op jit(solution)/shard_map/stack | solution.py:78
  106.3 16.8 %psum.14 = f32[5]{0:T(128)S(1)} all-reduce(f32[5]{0:T(128)S(1)} %stack.39), channel_id=1, replica_groups=mesh['gx'=4,'gy'=2,'gz'=4] {'gy','gz'}, use_global_device_ids=true, to_apply=%region_5.6 | all-reduce | flops 5 | bytes 40 | tf_op jit(solution)/shard_map/psum | solution.py:77
  123.1 10.9 %psum.15 = f32[5]{0:T(128)S(1)} all-reduce(f32[5]{0:T(128)S(1)} %psum.14), channel_id=1, replica_groups=mesh['gx'=4,'gy'=2,'gz'=4] {'gx'}, use_global_device_ids=true, to_apply=%region_6.7 | all-reduce | flops 5 | bytes 40 | tf_op jit(solution)/shard_map/psum | solution.py:77
  (106 shorter events, 24.3 us)
Async XLA Ops:
  1.5 6.8 %collective-permute-start = (f32[1,64,256]{2,1,0:T(8,128)S(1)}, f32[1,64,256]{2,1,0:T(8,128)S(1)}, u32[]{:S(2)}, u32[]{:S(2)}) collective-permute-start(f32[1,64,256]{2,1,0:T(8,128)S(1)} %slice.260), channel_id=1, source_target_pairs={{0,8},{8,16},{16,24},{1,9},{9,17},{17,25},{2,10},{10,18},{18,26},{... | collective-permute-start | bytes 196616 | tf_op jit(solution)/shard_map/ppermute | solution.py:13
  11.2 2.3 %copy-start = (f32[65,64,256]{2,1,0:T(8,128)}, f32[65,64,256]{2,1,0:T(8,128)S(1)}, u32[]{:S(2)}) copy-start(f32[65,64,256]{2,1,0:T(8,128)S(1)} %constant_dynamic-update-slice_fusion) | copy-start | bytes 12779524
  11.3 2.2 %collective-permute-start.1 = (f32[65,1,256]{2,1,0:T(1,128)S(1)}, f32[65,1,256]{2,1,0:T(1,128)S(1)}, u32[]{:S(2)}, u32[]{:S(2)}) collective-permute-start(f32[65,1,256]{2,1,0:T(1,128)S(1)} %slice.345), channel_id=1, source_target_pairs={{0,4},{1,5},{2,6},{3,7},{8,12},{9,13},{10,14},{11,15},{16,20},{17,... | collective-permute-start | bytes 199688 | tf_op jit(solution)/shard_map/ppermute | solution.py:13
  15.1 5.1 %collective-permute-start.2 = (f32[65,65,1]{1,2,0:T(1,128)S(1)}, f32[65,65,1]{1,2,0:T(1,128)S(1)}, u32[]{:S(2)}, u32[]{:S(2)}) collective-permute-start(f32[65,65,1]{1,2,0:T(1,128)S(1)} %copy.49), channel_id=1, source_target_pairs={{0,1},{1,2},{2,3},{4,5},{5,6},{6,7},{8,9},{9,10},{10,11},{12,13},{... | collective-permute-start | bytes 50708 | tf_op jit(solution)/shard_map/ppermute | solution.py:13
  21.1 5.4 %slice-start = ((s8[4259840]{0:T(1024)(128)(4,1)}), s8[4194304]{0:T(1024)(128)(4,1)S(1)}, s32[]{:S(2)}) async-start(s8[4259840]{0:T(1024)(128)(4,1)} %bitcast.208), calls=%async_computation | async-start | bytes 8388608
  25.8 0.8 slice-start.1
  35.9 5.7 %collective-permute-start.3 = (f32[1,32,128]{2,1,0:T(8,128)S(1)}, f32[1,32,128]{2,1,0:T(8,128)S(1)}, u32[]{:S(2)}, u32[]{:S(2)}) collective-permute-start(f32[1,32,128]{2,1,0:T(8,128)S(1)} %slice.357), channel_id=1, source_target_pairs={{0,8},{8,16},{16,24},{1,9},{9,17},{17,25},{2,10},{10,18},{18,26},{... | collective-permute-start | bytes 49160 | tf_op jit(solution)/shard_map/ppermute | solution.py:13
  41.6 2.1 %collective-permute-start.4 = (f32[33,1,128]{2,1,0:T(1,128)S(1)}, f32[33,1,128]{2,1,0:T(1,128)S(1)}, u32[]{:S(2)}, u32[]{:S(2)}) collective-permute-start(f32[33,1,128]{2,1,0:T(1,128)S(1)} %pad_maximum_fusion.9), channel_id=1, source_target_pairs={{0,4},{1,5},{2,6},{3,7},{8,12},{9,13},{10,14},{11,15},{16,20},{17,... | collective-permute-start | bytes 50696 | tf_op jit(solution)/shard_map/ppermute | solution.py:13
  44.3 5.7 %collective-permute-start.5 = (f32[33,33,1]{1,2,0:T(1,128)S(1)}, f32[33,33,1]{1,2,0:T(1,128)S(1)}, u32[]{:S(2)}, u32[]{:S(2)}) collective-permute-start(f32[33,33,1]{1,2,0:T(1,128)S(1)} %copy.58), channel_id=1, source_target_pairs={{0,1},{1,2},{2,3},{4,5},{5,6},{6,7},{8,9},{9,10},{10,11},{12,13},{... | collective-permute-start | bytes 13076 | tf_op jit(solution)/shard_map/ppermute | solution.py:13
  53.0 5.6 %collective-permute-start.6 = (f32[1,16,64]{2,1,0:T(8,128)S(1)}, f32[1,16,64]{2,1,0:T(8,128)S(1)}, u32[]{:S(2)}, u32[]{:S(2)}) collective-permute-start(f32[1,16,64]{2,1,0:T(8,128)S(1)} %slice.369), channel_id=1, source_target_pairs={{0,8},{8,16},{16,24},{1,9},{9,17},{17,25},{2,10},{10,18},{18,26},{... | collective-permute-start | bytes 12296 | tf_op jit(solution)/shard_map/ppermute | solution.py:13
  58.7 2.1 %collective-permute-start.7 = (f32[17,1,64]{2,1,0:T(1,128)S(1)}, f32[17,1,64]{2,1,0:T(1,128)S(1)}, u32[]{:S(2)}, u32[]{:S(2)}) collective-permute-start(f32[17,1,64]{2,1,0:T(1,128)S(1)} %pad_maximum_fusion.10), channel_id=1, source_target_pairs={{0,4},{1,5},{2,6},{3,7},{8,12},{9,13},{10,14},{11,15},{16,20},{17,... | collective-permute-start | bytes 13064 | tf_op jit(solution)/shard_map/ppermute | solution.py:13
  60.9 9.1 %collective-permute-start.8 = (f32[17,17,1]{2,1,0:T(8,128)S(1)}, f32[17,17,1]{2,1,0:T(8,128)S(1)}, u32[]{:S(2)}, u32[]{:S(2)}) collective-permute-start(f32[17,17,1]{2,1,0:T(8,128)S(1)} %pad_maximum_fusion.3), channel_id=1, source_target_pairs={{0,1},{1,2},{2,3},{4,5},{5,6},{6,7},{8,9},{9,10},{10,11},{12,13},{... | collective-permute-start | bytes 3476 | tf_op jit(solution)/shard_map/ppermute | solution.py:13
  71.3 6.4 %collective-permute-start.9 = (f32[1,8,32]{2,1,0:T(8,128)S(1)}, f32[1,8,32]{2,1,0:T(8,128)S(1)}, u32[]{:S(2)}, u32[]{:S(2)}) collective-permute-start(f32[1,8,32]{2,1,0:T(8,128)S(1)} %slice.381), channel_id=1, source_target_pairs={{0,8},{8,16},{16,24},{1,9},{9,17},{17,25},{2,10},{10,18},{18,26},{... | collective-permute-start | bytes 3080 | tf_op jit(solution)/shard_map/ppermute | solution.py:13
  77.7 2.1 %collective-permute-start.10 = (f32[9,1,32]{2,1,0:T(1,128)S(1)}, f32[9,1,32]{2,1,0:T(1,128)S(1)}, u32[]{:S(2)}, u32[]{:S(2)}) collective-permute-start(f32[9,1,32]{2,1,0:T(1,128)S(1)} %pad_maximum_fusion.11), channel_id=1, source_target_pairs={{0,4},{1,5},{2,6},{3,7},{8,12},{9,13},{10,14},{11,15},{16,20},{17,... | collective-permute-start | bytes 3464 | tf_op jit(solution)/shard_map/ppermute | solution.py:13
  79.9 6.4 %collective-permute-start.11 = (f32[9,9,1]{2,1,0:T(8,128)S(1)}, f32[9,9,1]{2,1,0:T(8,128)S(1)}, u32[]{:S(2)}, u32[]{:S(2)}) collective-permute-start(f32[9,9,1]{2,1,0:T(8,128)S(1)} %pad_maximum_fusion.5), channel_id=1, source_target_pairs={{0,1},{1,2},{2,3},{4,5},{5,6},{6,7},{8,9},{9,10},{10,11},{12,13},{... | collective-permute-start | bytes 980 | tf_op jit(solution)/shard_map/ppermute | solution.py:13
  87.5 6.4 %collective-permute-start.12 = (f32[1,4,16]{2,1,0:T(4,128)S(1)}, f32[1,4,16]{2,1,0:T(4,128)S(1)}, u32[]{:S(2)}, u32[]{:S(2)}) collective-permute-start(f32[1,4,16]{2,1,0:T(4,128)S(1)} %slice.393), channel_id=1, source_target_pairs={{0,8},{8,16},{16,24},{1,9},{9,17},{17,25},{2,10},{10,18},{18,26},{... | collective-permute-start | bytes 776 | tf_op jit(solution)/shard_map/ppermute | solution.py:13
  93.8 2.1 %collective-permute-start.13 = (f32[5,1,16]{2,1,0:T(1,128)S(1)}, f32[5,1,16]{2,1,0:T(1,128)S(1)}, u32[]{:S(2)}, u32[]{:S(2)}) collective-permute-start(f32[5,1,16]{2,1,0:T(1,128)S(1)} %pad_maximum_fusion.12), channel_id=1, source_target_pairs={{0,4},{1,5},{2,6},{3,7},{8,12},{9,13},{10,14},{11,15},{16,20},{17,... | collective-permute-start | bytes 968 | tf_op jit(solution)/shard_map/ppermute | solution.py:13
  96.0 5.9 %collective-permute-start.14 = (f32[5,5,1]{2,1,0:T(8,128)S(1)}, f32[5,5,1]{2,1,0:T(8,128)S(1)}, u32[]{:S(2)}, u32[]{:S(2)}) collective-permute-start(f32[5,5,1]{2,1,0:T(8,128)S(1)} %pad_maximum_fusion.7), channel_id=1, source_target_pairs={{0,1},{1,2},{2,3},{4,5},{5,6},{6,7},{8,9},{9,10},{10,11},{12,13},{... | collective-permute-start | bytes 308 | tf_op jit(solution)/shard_map/ppermute | solution.py:13
